TPU v7x, 32 devices: a whole 2x2x4 slice. The times are simulated.
32 devices in a mesh: scene: 2 (over x), view: 16 (over z, y, core).
Axes of the slice: x: 2, y: 2, z: 4, core: 2. Of those that a mesh axis runs over, the one named last changes fastest.
Arguments:
- latents: bfloat16 [256, 64, 512], P(('scene', 'view')), parts along dimension 0, may hold values from -48 to 48
- norm_gain: float32 [512], replicated, may hold values from 0.1 to 1.9
- norm_shift: float32 [512], replicated, may hold values from -3 to 3
- w_first: bfloat16 [512, 3, 3, 512], replicated, may hold values from -0.09375 to 0.09375
- bias_first: float32 [512], replicated, may hold values from -3 to 3
- w_second: bfloat16 [512, 3, 3, 512], replicated, may hold values from -0.09375 to 0.09375
- bias_second: float32 [512], replicated, may hold values from -3 to 3
Outputs:
- decoded: bfloat16 [512, 128, 512], P(('scene', 'view')), parts along dimension 0
There are 2 independent parts, one for each index of `scene`. A program takes and returns all parts, laid end to end along the dimension named above; an argument that names none is the same for every part. Nothing has to cross between parts.
All inputs are finite; a program needn't handle non-finite values.
Results may differ from a plain program's by a relative error of at most 0.0051.
Values may be sent and summed in bfloat16 or wider, within the bound.
A program may use at most 128 MiB of HBM per device.

v0:
```python
import jax
import jax.numpy as jnp
from jax import lax
from jax.sharding import PartitionSpec as P

GROUPS = 32
H_LAT = 32


epsilon = 1e-06


def shifted(block, axis, distance):
    devices = range(lax.axis_size(axis))
    route = [(i - distance, i) for i in devices if i - distance in devices]
    return lax.ppermute(block, axis, route)


def conv_taps(padded, filters, out_rows, out_cols):
    result = None
    for tap_row in range(3):
        for tap_col in range(3):
            window = padded[tap_row : tap_row + out_rows, tap_col : tap_col + out_cols, :]
            term = jnp.einsum(
                "rwi,oi->rwo",
                window,
                filters[:, tap_row, tap_col, :],
                preferred_element_type=jnp.float32,
            )
            result = term if result is None else result + term
    return result


def pad_columns(block):
    return jnp.pad(block, ((0, 0), (1, 1), (0, 0)))


def keep_inside(block, first_row):
    position = first_row + jnp.arange(block.shape[0], dtype=jnp.int32)
    inside = (position >= 0) & (position < H_LAT)
    return jnp.where(inside[:, None, None], block, jnp.zeros((), block.dtype))


def spread_channels(group_values, channels):
    return jnp.broadcast_to(group_values[:, None], (GROUPS, channels // GROUPS)).reshape(channels)


def group_total(channel_values, channels):
    return jnp.sum(channel_values.reshape(GROUPS, channels // GROUPS), axis=1)


def per_device(latents, norm_gain, norm_shift, w_first, bias_first, w_second, bias_second):
    slab_rows, columns, channels = latents.shape
    slab_count = H_LAT // slab_rows
    view_count = lax.axis_size("view") // slab_count
    slab_index = lax.axis_index("view") // view_count
    slab_start = slab_index * slab_rows
    entries = float(slab_rows * columns * (channels // GROUPS) * lax.axis_size("view"))
    values = latents.astype(jnp.float32)
    group_sums = group_total(jnp.sum(values, axis=(0, 1)), channels)
    group_squares = group_total(jnp.sum(values * values, axis=(0, 1)), channels)
    total_sums, total_squares = lax.psum((group_sums, group_squares), "view")
    group_mean = total_sums / entries
    group_var = total_squares / entries - group_mean * group_mean
    channel_scale = spread_channels(lax.rsqrt(group_var + epsilon), channels) * norm_gain
    channel_offset = norm_shift - spread_channels(group_mean, channels) * channel_scale
    above = shifted(latents[-1:], "view", view_count)
    below = shifted(latents[:1], "view", -view_count)
    edged = jnp.concatenate([above, latents, below], axis=0)
    active = keep_inside(
        jax.nn.silu(edged.astype(jnp.float32) * channel_scale + channel_offset).astype(
            jnp.bfloat16
        ),
        slab_start - 1,
    )
    filtered = conv_taps(pad_columns(active), w_first, slab_rows, columns)
    own_mixed = (values + filtered + bias_first).astype(jnp.bfloat16)
    mixed_top = shifted(own_mixed[-1:], "view", view_count)
    mixed_bottom = shifted(own_mixed[:1], "view", -view_count)
    mixed = jnp.concatenate([mixed_top, own_mixed, mixed_bottom], axis=0)
    mixed = keep_inside(mixed, slab_start - 1)
    tall_rows = mixed.shape[0]
    doubled = jnp.broadcast_to(mixed[:, None, :, None, :], (tall_rows, 2, columns, 2, channels))
    doubled = doubled.reshape(2 * tall_rows, 2 * columns, channels)
    doubled = doubled[1 : 2 * slab_rows + 3]
    decoded = conv_taps(pad_columns(doubled), w_second, 2 * slab_rows, 2 * columns) + bias_second
    return decoded.astype(jnp.bfloat16)


def solution(mesh):
    placed = (P(("scene", "view"), None, None), P(), P(), P(), P(), P(), P())
    return jax.shard_map(
        per_device,
        mesh=mesh,
        in_specs=placed,
        out_specs=P(("scene", "view"), None, None),
        check_vma=False,
    )
```

profile of v0, /device:TPU:0, one launch (start us, length us, event | category | flops | bytes accessed | tf_op | source)
XLA Modules:
  0.0 113.7 jit_solution(12478874784361860435)
XLA Ops:
  0.0 0.9 fusion.97
  0.9 5.0 %collective-permute-start = (bf16[1,64,512]{2,1,0:T(8,128)(2,1)S(1)}, bf16[1,64,512]{2,1,0:T(8,128)(2,1)S(1)}, u32[]{:S(2)}, u32[]{:S(2)}) collective-permute-start(bf16[1,64,512]{2,1,0:T(8,128)(2,1)S(1)} %get-tuple-element.13), channel_id=1, source_target_pairs={{0,4},{1,5},{2,6},{3,7},{4,8},{5,9},{6,10},{7,11},{8,12},{9,13},{1... | collective-permute-start | bytes 196616 | tf_op jit(solution)/shard_map/ppermute | solution.py:16
  5.9 1.3 %collective-permute-start.1 = (bf16[1,64,512]{2,1,0:T(8,128)(2,1)S(1)}, bf16[1,64,512]{2,1,0:T(8,128)(2,1)S(1)}, u32[]{:S(2)}, u32[]{:S(2)}) collective-permute-start(bf16[1,64,512]{2,1,0:T(8,128)(2,1)S(1)} %get-tuple-element.14), channel_id=1, source_target_pairs={{4,0},{5,1},{6,2},{7,3},{8,4},{9,5},{10,6},{11,7},{12,8},{13,9},{1... | collective-permute-start | bytes 196616 | tf_op jit(solution)/shard_map/ppermute | solution.py:16
  7.2 1.2 %fusion.23 = (f32[512]{0:T(512)S(1)}, f32[512]{0:T(512)S(1)}) fusion(bf16[8,64,512]{2,1,0:T(8,128)(2,1)} %param.7), kind=kLoop, calls=%fused_computation.33 | loop fusion | flops 1047552 | bytes 528384 | tf_op jit(solution)/shard_map/reduce_sum | solution.py:61
  8.4 0.1 reshape.78
  8.5 0.1 reshape.79
  8.5 0.1 reduce_sum.37
  8.7 0.1 reduce_sum.39
  8.8 34.0 %all-reduce.2 = (f32[32]{0:T(128)S(1)}, f32[32]{0:T(128)S(1)}) all-reduce(f32[32]{0:T(128)S(1)} %reduce_sum.39, f32[32]{0:T(128)S(1)} %reduce_sum.37), channel_id=1, replica_groups=mesh['scene'=2,'view'=16] {'view'}, use_global_device_ids=true, to_apply=%region_5.6 | all-reduce | flops 64 | bytes 512 | tf_op jit(solution)/shard_map/psum | solution.py:62
  42.8 0.1 broadcast_in_dim.47
  42.8 0.1 reshape.80
  42.9 0.1 broadcast_in_dim.48
  43.0 0.1 reshape.81
  43.1 0.7 multiply_subtract_fusion
  43.8 1.6 %fusion.24 = bf16[10,64,512]{2,1,0:T(8,128)(2,1)S(1)} fusion(bf16[1,64,512]{2,1,0:T(8,128)(2,1)S(1)} %collective-permute-done.1, bf16[8,64,512]{2,1,0:T(8,128)(2,1)} %param.7, bf16[1,64,512]{2,1,0:T(8,128)(2,1)S(1)} %collective-permute-done, f32[512]{0:T(512)S(1)} %get-tuple-element.9, f32[512]{0:T(512)S(1)} %get-tuple-element.10, ...), kind=kLoop, calls=%fused_computation.34 | loop fusion | flops 3604480 | bytes 1314826 | tf_op jit(solution)/shard_map/jit(_where)/select_n | solution.py:41
  45.5 1.5 %fusion.38 = f32[8,64,512]{2,1,0:T(8,128)S(1)} fusion(bf16[512,3,3,512]{3,0,2,1:T(8,128)(2,1)} %param.10, bf16[10,64,512]{2,1,0:T(8,128)(2,1)S(1)} %fusion.24), kind=kOutput, calls=%fused_computation.51 | convolution fusion | flops 268435456 | bytes 2228224 | tf_op jit(solution)/shard_map/rwi,oi->rwo/dot_general | solution.py:24
  47.0 1.5 %fusion.46 = f32[8,64,512]{2,1,0:T(8,128)S(1)} fusion(bf16[512,3,3,512]{3,0,2,1:T(8,128)(2,1)} %param.10, bf16[10,64,512]{2,1,0:T(8,128)(2,1)S(1)} %fusion.24), kind=kOutput, calls=%fused_computation.59 | convolution fusion | flops 268435456 | bytes 2228224 | tf_op jit(solution)/shard_map/rwi,oi->rwo/dot_general | solution.py:24
  48.5 0.5 fusion.42
  49.0 0.5 fusion.49
  49.5 0.1 copy-done.1
  49.6 0.5 fusion.20
  50.1 0.5 convolution_add_fusion.4
  50.5 0.5 fusion.19
  51.1 0.5 convolution_add_fusion.3
  51.5 0.2 copy-done.4
  51.7 0.6 fusion.22
  52.3 1.3 %collective-permute-start.2 = (bf16[1,64,512]{2,1,0:T(8,128)(2,1)S(1)}, bf16[1,64,512]{2,1,0:T(8,128)(2,1)S(1)}, u32[]{:S(2)}, u32[]{:S(2)}) collective-permute-start(bf16[1,64,512]{2,1,0:T(8,128)(2,1)S(1)} %get-tuple-element.11), channel_id=1, source_target_pairs={{0,4},{1,5},{2,6},{3,7},{4,8},{5,9},{6,10},{7,11},{8,12},{9,13},{1... | collective-permute-start | bytes 196616 | tf_op jit(solution)/shard_map/ppermute | solution.py:16
  53.6 1.3 %collective-permute-start.3 = (bf16[1,64,512]{2,1,0:T(8,128)(2,1)S(1)}, bf16[1,64,512]{2,1,0:T(8,128)(2,1)S(1)}, u32[]{:S(2)}, u32[]{:S(2)}) collective-permute-start(bf16[1,64,512]{2,1,0:T(8,128)(2,1)S(1)} %get-tuple-element.12), channel_id=1, source_target_pairs={{4,0},{5,1},{6,2},{7,3},{8,4},{9,5},{10,6},{11,7},{12,8},{13,9},{1... | collective-permute-start | bytes 196616 | tf_op jit(solution)/shard_map/ppermute | solution.py:16
  54.9 0.1 slice.185
  55.0 0.5 collective-permute-done.2
  55.5 4.3 %collective-permute-done.3 = bf16[1,64,512]{2,1,0:T(8,128)(2,1)S(1)} collective-permute-done((bf16[1,64,512]{2,1,0:T(8,128)(2,1)S(1)}, bf16[1,64,512]{2,1,0:T(8,128)(2,1)S(1)}, u32[]{:S(2)}, u32[]{:S(2)}) %collective-permute-start.3) | collective-permute-done | bytes 65568 | tf_op jit(solution)/shard_map/ppermute | solution.py:16
  59.8 0.1 maximum_select_fusion
  59.9 3.5 %broadcast_in_dim.50 = bf16[10,2,64,2,512]{4,3,2,1,0:T(2,128)(2,1)} broadcast(bf16[10,64,512]{2,1,0:T(8,128)(2,1)S(1)} %maximum_select_fusion), dimensions={0,2,4} | broadcast | bytes 3276800 | tf_op jit(solution)/shard_map/broadcast_in_dim | solution.py:83
  63.4 3.8 %reshape.82 = bf16[20,128,512]{2,1,0:T(8,128)(2,1)S(1)} reshape(bf16[10,2,64,2,512]{4,3,2,1,0:T(2,128)(2,1)} %broadcast_in_dim.50) | data formatting | bytes 5242880 | tf_op jit(solution)/shard_map/reshape | solution.py:84
  67.2 0.2 slice.184
  67.4 0.0 slice-start.1
  67.4 4.4 %fusion.8 = f32[16,128,512]{2,1,0:T(8,128)} fusion(bf16[18,128,512]{2,1,0:T(8,128)(2,1)S(1)} %slice.184, bf16[512,3,3,512]{3,0,2,1:T(8,128)(2,1)} %param.12), kind=kOutput, calls=%fused_computation.9 | convolution fusion | flops 1073741824 | bytes 7077888 | tf_op jit(solution)/shard_map/rwi,oi->rwo/dot_general | solution.py:24
  71.8 4.3 %fusion.6 = f32[16,128,512]{2,1,0:T(8,128)} fusion(bf16[18,128,512]{2,1,0:T(8,128)(2,1)S(1)} %slice.184, bf16[512,3,3,512]{3,0,2,1:T(8,128)(2,1)} %param.12), kind=kOutput, calls=%fused_computation.7 | convolution fusion | flops 1073741824 | bytes 7077888 | tf_op jit(solution)/shard_map/rwi,oi->rwo/dot_general | solution.py:24
  76.1 3.2 %fusion.4 = f32[16,128,512]{2,1,0:T(8,128)} fusion(bf16[18,128,512]{2,1,0:T(8,128)(2,1)S(1)} %slice.184, bf16[512,3,3,512]{3,0,2,1:T(8,128)(2,1)S(1)} %bitcast.101), kind=kOutput, calls=%fused_computation.5 | convolution fusion | flops 1073741824 | bytes 7077888 | tf_op jit(solution)/shard_map/rwi,oi->rwo/dot_general | solution.py:24
  79.3 3.3 %fusion.2 = f32[16,128,512]{2,1,0:T(8,128)} fusion(bf16[18,128,512]{2,1,0:T(8,128)(2,1)S(1)} %slice.184, bf16[512,3,3,512]{3,0,2,1:T(8,128)(2,1)S(1)} %bitcast.101), kind=kOutput, calls=%fused_computation.3 | convolution fusion | flops 1073741824 | bytes 7077888 | tf_op jit(solution)/shard_map/rwi,oi->rwo/dot_general | solution.py:24
  82.6 3.2 %fusion = f32[16,128,512]{2,1,0:T(8,128)} fusion(bf16[18,128,512]{2,1,0:T(8,128)(2,1)S(1)} %slice.184, bf16[512,3,3,512]{3,0,2,1:T(8,128)(2,1)S(1)} %bitcast.101), kind=kOutput, calls=%fused_computation.1 | convolution fusion | flops 1073741824 | bytes 7077888 | tf_op jit(solution)/shard_map/rwi,oi->rwo/dot_general | solution.py:24
  85.9 3.3 %fusion.10 = f32[16,128,512]{2,1,0:T(8,128)} fusion(bf16[18,128,512]{2,1,0:T(8,128)(2,1)S(1)} %slice.184, bf16[512,3,3,512]{3,0,2,1:T(8,128)(2,1)S(1)} %bitcast.101), kind=kOutput, calls=%fused_computation.11 | convolution fusion | flops 1073741824 | bytes 7077888 | tf_op jit(solution)/shard_map/rwi,oi->rwo/dot_general | solution.py:24
  89.1 3.2 %fusion.35 = f32[16,128,512]{2,1,0:T(8,128)} fusion(bf16[20,128,512]{2,1,0:T(8,128)(2,1)S(1)} %reshape.82, bf16[512,3,3,512]{3,0,2,1:T(8,128)(2,1)S(1)} %bitcast.101), kind=kOutput, calls=%fused_computation.48 | convolution fusion | flops 1073741824 | bytes 7340032 | tf_op jit(solution)/shard_map/rwi,oi->rwo/dot_general | solution.py:24
  92.4 0.1 fusion.26
  92.5 2.9 %broadcast_in_dim.53 = bf16[8,2,64,2,512]{4,3,2,1,0:T(2,128)(2,1)} broadcast(bf16[8,64,512]{2,1,0:T(8,128)(2,1)S(1)} %fusion.26), dimensions={0,2,4} | broadcast | bytes 2621440 | tf_op jit(solution)/shard_map/broadcast_in_dim | solution.py:83
  95.4 4.1 %slice.172 = bf16[16,128,512]{2,1,0:T(8,128)(2,1)} reshape(bf16[8,2,64,2,512]{4,3,2,1,0:T(2,128)(2,1)} %broadcast_in_dim.53) | data formatting | bytes 4194304 | tf_op jit(solution)/shard_map/slice | solution.py:23
  99.6 3.1 %fusion.31 = f32[16,128,512]{2,1,0:T(8,128)S(1)} fusion(bf16[16,128,512]{2,1,0:T(8,128)(2,1)} %slice.172, bf16[512,3,3,512]{3,0,2,1:T(8,128)(2,1)} %param.12), kind=kOutput, calls=%fused_computation.44 | convolution fusion | flops 1073741824 | bytes 6815744 | tf_op jit(solution)/shard_map/rwi,oi->rwo/dot_general | solution.py:24
  102.7 11.0 %add_convert_fusion = bf16[16,128,512]{2,1,0:T(8,128)(2,1)} fusion(f32[16,128,512]{2,1,0:T(8,128)} %fusion, f32[16,128,512]{2,1,0:T(8,128)} %fusion.2, f32[16,128,512]{2,1,0:T(8,128)} %fusion.4, f32[16,128,512]{2,1,0:T(8,128)S(1)} %fusion.31, f32[16,128,512]{2,1,0:T(8,128)} %fusion.6, f32[16,128,512]{2,1,0:T(8,128)S(1)} %copy-done, ...), kind=kOutput, calls=%fused_computation | convolution fusion | flops 1084227584 | bytes 38799360 | tf_op jit(solution)/shard_map/rwi,oi->rwo/dot_general | solution.py:24
  (17 shorter events, 0.1 us)
Async XLA Ops:
  0.9 42.9 %collective-permute-start = (bf16[1,64,512]{2,1,0:T(8,128)(2,1)S(1)}, bf16[1,64,512]{2,1,0:T(8,128)(2,1)S(1)}, u32[]{:S(2)}, u32[]{:S(2)}) collective-permute-start(bf16[1,64,512]{2,1,0:T(8,128)(2,1)S(1)} %get-tuple-element.13), channel_id=1, source_target_pairs={{0,4},{1,5},{2,6},{3,7},{4,8},{5,9},{6,10},{7,11},{8,12},{9,13},{1... | collective-permute-start | bytes 196616 | tf_op jit(solution)/shard_map/ppermute | solution.py:16
  5.9 38.0 %collective-permute-start.1 = (bf16[1,64,512]{2,1,0:T(8,128)(2,1)S(1)}, bf16[1,64,512]{2,1,0:T(8,128)(2,1)S(1)}, u32[]{:S(2)}, u32[]{:S(2)}) collective-permute-start(bf16[1,64,512]{2,1,0:T(8,128)(2,1)S(1)} %get-tuple-element.14), channel_id=1, source_target_pairs={{4,0},{5,1},{6,2},{7,3},{8,4},{9,5},{10,6},{11,7},{12,8},{13,9},{1... | collective-permute-start | bytes 196616 | tf_op jit(solution)/shard_map/ppermute | solution.py:16
  43.8 4.7 %copy-start.2 = (bf16[512,3,3,512]{3,0,2,1:T(8,128)(2,1)S(1)}, bf16[512,3,3,512]{3,0,2,1:T(8,128)(2,1)}, u32[]{:S(2)}) copy-start(bf16[512,3,3,512]{3,0,2,1:T(8,128)(2,1)} %param.10) | copy-start | bytes 14155780
  48.5 1.0 copy-start.1
  51.0 0.7 copy-start.4
  52.3 3.2 %collective-permute-start.2 = (bf16[1,64,512]{2,1,0:T(8,128)(2,1)S(1)}, bf16[1,64,512]{2,1,0:T(8,128)(2,1)S(1)}, u32[]{:S(2)}, u32[]{:S(2)}) collective-permute-start(bf16[1,64,512]{2,1,0:T(8,128)(2,1)S(1)} %get-tuple-element.11), channel_id=1, source_target_pairs={{0,4},{1,5},{2,6},{3,7},{4,8},{5,9},{6,10},{7,11},{8,12},{9,13},{1... | collective-permute-start | bytes 196616 | tf_op jit(solution)/shard_map/ppermute | solution.py:16
  53.6 6.2 %collective-permute-start.3 = (bf16[1,64,512]{2,1,0:T(8,128)(2,1)S(1)}, bf16[1,64,512]{2,1,0:T(8,128)(2,1)S(1)}, u32[]{:S(2)}, u32[]{:S(2)}) collective-permute-start(bf16[1,64,512]{2,1,0:T(8,128)(2,1)S(1)} %get-tuple-element.12), channel_id=1, source_target_pairs={{4,0},{5,1},{6,2},{7,3},{8,4},{9,5},{10,6},{11,7},{12,8},{13,9},{1... | collective-permute-start | bytes 196616 | tf_op jit(solution)/shard_map/ppermute | solution.py:16
  67.2 8.9 %slice-start = ((s8[4718592]{0:T(1024)(128)(4,1)}), s8[4194304]{0:T(1024)(128)(4,1)S(1)}, s32[]{:S(2)}) async-start(s8[4718592]{0:T(1024)(128)(4,1)} %bitcast.100), calls=%async_computation | async-start | bytes 8388608
  67.4 8.7 %slice-start.1 = ((s8[4718592]{0:T(1024)(128)(4,1)}), s8[524288]{0:T(1024)(128)(4,1)S(1)}, s32[]{:S(2)}) async-start(s8[4718592]{0:T(1024)(128)(4,1)} %bitcast.100), calls=%async_computation.1 | async-start | bytes 1048576
  99.6 3.1 %copy-start = (f32[16,128,512]{2,1,0:T(8,128)S(1)}, f32[16,128,512]{2,1,0:T(8,128)}, u32[]{:S(2)}) copy-start(f32[16,128,512]{2,1,0:T(8,128)} %fusion.8) | copy-start | bytes 12582916
  99.6 3.1 %copy-start.3 = (f32[512]{0:T(512)S(1)}, f32[512]{0:T(512)}, u32[]{:S(2)}) copy-start(f32[512]{0:T(512)} %param.13) | copy-start | bytes 6148
where the time goes:
time: 114 us
  matrix products  45.6 us (40%)
  blocking collectives  34 us (30%)
  local copies, waits for them, and re-layouts  16.2 us (14%)
  starting transfers between devices  8.84 us (8%)
  waiting for transfers between devices  4.79 us (4%)
  other arithmetic  4.04 us (4%)
    dot_general x18, matrix products, conv_taps(): jnp.einsum('rwi,oi->rwo', window, filters[:, tap_row, tap_col, :], prefer...  45.6 us
    psum x1, blocking collectives, per_device(): total_sums, total_squares = lax.psum((group_sums, group_squares), 'view')  34 us
    ppermute x4, starting transfers between devices, shifted(): return lax.ppermute(block, axis, route)  8.84 us
    broadcast_in_dim x2, local copies, waits for them, and re-layouts, per_device(): jnp.broadcast_to(mixed[:, None, :, None, :], (tall_rows, 2, columns, 2, c...  6.43 us
    ppermute x4, waiting for transfers between devices, shifted(): return lax.ppermute(block, axis, route)  4.79 us
    slice x2, local copies, waits for them, and re-layouts, conv_taps(): window = padded[tap_row:tap_row + out_rows, tap_col:tap_col + out_cols, :]  4.19 us
    reshape x1, local copies, waits for them, and re-layouts, per_device(): doubled = doubled.reshape(2 * tall_rows, 2 * columns, channels)  3.75 us
  transfers between devices with their start and end apart: 4, of which 2 were waited for; matrix products, arithmetic and copies ran while one was open for 2% of the time, Pallas kernels for 0%

commit v1 on v0

v1 whole, which is shorter than its diff:
```python
import functools

import jax
import jax.numpy as jnp
from jax import lax
from jax.experimental import pallas as pl
from jax.experimental.pallas import tpu as pltpu
from jax.sharding import PartitionSpec as P

GROUPS = 32
H_LAT = 32
EPSILON = 1e-06
LANES = 128
F32 = jnp.float32
BF16 = jnp.bfloat16


def dot_nt(x, w):
    return lax.dot_general(x, w, (((1,), (1,)), ((), ())), preferred_element_type=F32)


def kernel(
    n_view, rows, cols, chans,
    lat_hbm, gain_ref, shift_ref, w1_hbm, b1_ref, w2_hbm, b2_ref,
    out_ref,
    lat, w1, w2, fold, act, acc, lhs_m, lhs_u, part, wide, stat, stat_in,
    lat_sem, w1_sem, w2_sem, halo_send, halo_recv, stat_send, stat_recv,
):
    me = lax.axis_index("view")
    slabs = H_LAT // rows
    views = n_view // slabs
    slab = me // views
    own = rows * cols
    ext = (rows + 2) * cols
    has_up = slab > 0
    has_down = slab < slabs - 1

    own_copy = pltpu.make_async_copy(lat_hbm, lat.at[pl.ds(2, rows)], lat_sem)
    own_copy.start()

    barrier = pltpu.get_barrier_semaphore()

    def greet(k, carry):
        pl.semaphore_signal(barrier, inc=1, device_id={"view": lax.rem(me + k, n_view)})
        return carry

    lax.fori_loop(1, n_view, greet, 0)

    def w1_copy(t):
        return pltpu.make_async_copy(w1_hbm.at[t], w1.at[t], w1_sem.at[t])

    def w2_copy(t):
        return pltpu.make_async_copy(w2_hbm.at[t], w2.at[t], w2_sem.at[t])

    for t in range(9):
        w1_copy(t).start()
    for t in range(9):
        w2_copy(t).start()

    own_copy.wait()

    def add_row(i, carry):
        x = lat[2 + i].astype(F32).reshape(cols // 8, 8, chans)
        return carry[0] + jnp.sum(x, axis=0), carry[1] + jnp.sum(x * x, axis=0)

    zero = jnp.zeros((8, chans), F32)
    sums, squares = lax.fori_loop(0, rows, add_row, (zero, zero))
    sums = jnp.sum(sums, axis=0, keepdims=True)
    squares = jnp.sum(squares, axis=0, keepdims=True)
    blocks = chans // LANES
    packed = jnp.concatenate(
        [v[:, k * LANES : (k + 1) * LANES] for v in (sums, squares) for k in range(blocks)], axis=0
    )
    lane = lax.broadcasted_iota(jnp.int32, packed.shape, 1)
    step = 1
    while step < chans // GROUPS:
        packed = packed + jnp.where(
            (lane & step) == 0,
            pltpu.roll(packed, LANES - step, 1),
            pltpu.roll(packed, step, 1),
        )
        step *= 2
    stat[...] = packed

    pl.semaphore_wait(barrier, n_view - 1)

    def stat_copy(k):
        return pltpu.make_async_remote_copy(
            src_ref=stat, dst_ref=stat_in.at[k - 1], send_sem=stat_send, recv_sem=stat_recv,
            device_id={"view": lax.rem(me + k, n_view)},
        )

    def send_stat(k, carry):
        stat_copy(k).start()
        return carry

    lax.fori_loop(1, n_view, send_stat, 0)

    up_copy = pltpu.make_async_remote_copy(
        src_ref=lat_hbm.at[pl.ds(0, 2)], dst_ref=lat.at[pl.ds(rows + 2, 2)],
        send_sem=halo_send.at[0], recv_sem=halo_recv.at[0],
        device_id={"view": jnp.maximum(me - views, 0)},
    )
    down_copy = pltpu.make_async_remote_copy(
        src_ref=lat_hbm.at[pl.ds(rows - 2, 2)], dst_ref=lat.at[pl.ds(0, 2)],
        send_sem=halo_send.at[1], recv_sem=halo_recv.at[1],
        device_id={"view": jnp.minimum(me + views, n_view - 1)},
    )

    @pl.when(has_up)
    def _():
        up_copy.start()

    @pl.when(has_down)
    def _():
        down_copy.start()

    pltpu.make_async_copy(stat_in, stat_in, stat_recv).wait()

    total = stat[...]
    total = total + jnp.sum(stat_in[...], axis=0)
    entries = float(own * (chans // GROUPS) * n_view)
    mean = total[:blocks] / entries
    var = total[blocks:] / entries - mean * mean
    inv = lax.rsqrt(var + EPSILON)

    def one_row(v):
        return jnp.concatenate([v[k : k + 1] for k in range(blocks)], axis=1)

    scale = one_row(inv) * gain_ref[...]
    offset = shift_ref[...] - one_row(mean) * scale

    @pl.when(has_up)
    def _():
        down_copy.wait_recv()

    @pl.when(has_down)
    def _():
        up_copy.wait_recv()

    col = lax.broadcasted_iota(jnp.int32, (cols, chans), 0)

    def left_of(x):
        return jnp.where(col == 0, 0.0, pltpu.roll(x, 1, 0))

    def right_of(x):
        return jnp.where(col == cols - 1, 0.0, pltpu.roll(x, cols - 1, 0))

    half_scale = scale * 0.5
    half_offset = offset * 0.5

    def activate(i, carry):
        h = lat[i].astype(F32) * half_scale + half_offset
        a = h + h * jnp.tanh(h)
        place = slab * rows + i - 2
        a = jnp.where(jnp.logical_and(place >= 0, place < H_LAT), a, 0.0)
        at = pl.ds(pl.multiple_of(i * cols, cols), cols)
        act[0, at] = left_of(a).astype(BF16)
        act[1, at] = a.astype(BF16)
        act[2, at] = right_of(a).astype(BF16)
        return carry

    lax.fori_loop(0, rows + 4, activate, 0)

    def tap(t, carry):
        w1_copy(t).wait()
        r = t // 3
        s = t - 3 * r
        x = act[s, pl.ds(pl.multiple_of(r * cols, cols), ext)]
        term = dot_nt(x, w1[t])

        @pl.when(t == 0)
        def _():
            acc[...] = term

        @pl.when(t > 0)
        def _():
            acc[...] += term

        return carry

    lax.fori_loop(0, 9, tap, 0)

    for t in range(9):
        w2_copy(t).wait()
    piece = 32

    def fold_piece(k, carry):
        at = pl.ds(pl.multiple_of(k * piece, piece), piece)
        w = [w2[t, at].astype(F32) for t in range(9)]
        by_col = [w[s] + w[3 + s] + w[6 + s] for s in range(3)]
        fold[0, at] = (by_col[0] + by_col[1] + by_col[2]).astype(BF16)
        fold[1, at] = by_col[0].astype(BF16)
        fold[2, at] = by_col[2].astype(BF16)
        fold[3, at] = (w[0] + w[1] + w[2]).astype(BF16)
        fold[4, at] = (w[6] + w[7] + w[8]).astype(BF16)
        return carry

    lax.fori_loop(0, chans // piece, fold_piece, 0)

    bias1 = b1_ref[...]

    def mixed_row(i):
        at = pl.ds(pl.multiple_of(i * cols, cols), cols)
        m = lat[i + 1].astype(F32) + acc[at] + bias1
        m = m.astype(BF16).astype(F32)
        place = slab * rows + i - 1
        return jnp.where(jnp.logical_and(place >= 0, place < H_LAT), m, 0.0)

    def spread(i, carry):
        m = mixed_row(i + 1)
        u = m - mixed_row(i)
        at = pl.ds(pl.multiple_of(i * cols, cols), cols)
        for ref, x in ((lhs_m, m), (lhs_u, u)):
            ref[0, at] = x.astype(BF16)
            ref[1, at] = (left_of(x) - x).astype(BF16)
            ref[2, at] = (right_of(x) - x).astype(BF16)
        return carry

    lax.fori_loop(0, rows + 1, spread, 0)

    width = 256

    def out_tile(n, carry):
        lanes = pl.ds(pl.multiple_of(n * width, width), width)
        head = pl.ds(0, own)
        base = dot_nt(lhs_m[0, head], fold[0, lanes]) + b2_ref[:, lanes]
        part[0] = base + dot_nt(lhs_m[1, head], fold[1, lanes])
        part[1] = base + dot_nt(lhs_m[2, head], fold[2, lanes])
        for p in range(2):
            at = pl.ds(p * cols, own)
            rise = dot_nt(lhs_u[0, at], fold[3 + p, lanes])
            for q in range(2):
                term = rise + dot_nt(lhs_u[1 + q, at], w2[6 * p + 2 * q, lanes])
                value = part[q] + term if p else part[q] - term
                for g in range(width // LANES):
                    wide[g, pl.ds(p * own * 2 + q, own, 2), :] = value[:, g * LANES : (g + 1) * LANES]
        for p in range(2):
            for g in range(width // LANES):
                tile = wide[g, pl.ds(p * own * 2, own * 2), :].astype(BF16)
                out_ref[:, p, :, pl.ds(pl.multiple_of(n * width + g * LANES, LANES), LANES)] = tile.reshape(
                    rows, 2 * cols, LANES
                )
        return carry

    lax.fori_loop(0, chans // width, out_tile, 0)

    pltpu.make_async_copy(stat_in, stat_in, stat_send).wait()

    @pl.when(has_up)
    def _():
        up_copy.wait_send()

    @pl.when(has_down)
    def _():
        down_copy.wait_send()


def per_device(n_view, latents, norm_gain, norm_shift, w_first, bias_first, w_second, bias_second):
    rows, cols, chans = latents.shape
    own = rows * cols
    flat = lambda w: jnp.transpose(w, (1, 2, 0, 3)).reshape(9, chans, chans)
    row = lambda v: v.reshape(1, chans)
    vmem = pl.BlockSpec(memory_space=pltpu.VMEM)
    hbm = pl.BlockSpec(memory_space=pl.ANY)
    out = pl.pallas_call(
        functools.partial(kernel, n_view, rows, cols, chans),
        out_shape=jax.ShapeDtypeStruct((rows, 2, 2 * cols, chans), BF16),
        in_specs=[hbm, vmem, vmem, hbm, vmem, hbm, vmem],
        out_specs=vmem,
        scratch_shapes=[
            pltpu.VMEM((rows + 4, cols, chans), BF16),
            pltpu.VMEM((9, chans, chans), BF16),
            pltpu.VMEM((9, chans, chans), BF16),
            pltpu.VMEM((5, chans, chans), BF16),
            pltpu.VMEM((3, (rows + 4) * cols, chans), BF16),
            pltpu.VMEM(((rows + 2) * cols, chans), F32),
            pltpu.VMEM((3, own + cols, chans), BF16),
            pltpu.VMEM((3, own + cols, chans), BF16),
            pltpu.VMEM((2, own, 256), F32),
            pltpu.VMEM((2, own * 4, LANES), F32),
            pltpu.VMEM((2 * chans // LANES, LANES), F32),
            pltpu.VMEM((n_view - 1, 2 * chans // LANES, LANES), F32),
            pltpu.SemaphoreType.DMA,
            pltpu.SemaphoreType.DMA((9,)),
            pltpu.SemaphoreType.DMA((9,)),
            pltpu.SemaphoreType.DMA((2,)),
            pltpu.SemaphoreType.DMA((2,)),
            pltpu.SemaphoreType.DMA,
            pltpu.SemaphoreType.DMA,
        ],
        compiler_params=pltpu.CompilerParams(
            collective_id=0, has_side_effects=True, vmem_limit_bytes=60 * 1024 * 1024
        ),
    )(
        latents, row(norm_gain), row(norm_shift), flat(w_first), row(bias_first), flat(w_second),
        row(bias_second),
    )
    return out.reshape(2 * rows, 2 * cols, chans)


def solution(mesh):
    placed = (P(("scene", "view"), None, None), P(), P(), P(), P(), P(), P())
    return jax.shard_map(
        functools.partial(per_device, mesh.shape["view"]),
        mesh=mesh,
        in_specs=placed,
        out_specs=P(("scene", "view"), None, None),
        check_vma=False,
    )
```

time: 114 us -> 29 us (0.25)
  matrix products: 45.6 us -> 0 us
  blocking collectives: 34 us -> 0 us
  Pallas kernels: 0 us -> 25.7 us
  local copies, waits for them, and re-layouts: 16.2 us -> 3.1 us
  starting transfers between devices: 8.84 us -> 0 us
  waiting for transfers between devices: 4.79 us -> 0 us
  other arithmetic: 4.04 us -> 0 us
    dot_general x18 -> x0, matrix products: 45.6 us -> none  [conv_taps(): jnp.einsum('rwi,oi->rwo', window, filters[:, tap_row, tap_col, :], prefer...]
    psum x1 -> x0, blocking collectives: 34 us -> none  [per_device(): total_sums, total_squares = lax.psum((group_sums, group_squares), 'view')]
    pallas_call x0 -> x1, Pallas kernels: none -> 25.7 us  [per_device(): pl.pallas_call(functools.partial(kernel, n_view, rows, cols, chans), out_...]
    ppermute x4 -> x0, starting transfers between devices: 8.84 us -> none  [shifted(): return lax.ppermute(block, axis, route)]
    broadcast_in_dim x4 -> x0, local copies, waits for them, and re-layouts: 6.58 us -> none  [the longest x2 6.43 us: per_device(): jnp.broadcast_to(mixed[:, None, :, None, :], (tall_rows, 2, columns, 2, c...]
    slice x5 -> x0, local copies, waits for them, and re-layouts: 5.23 us -> none  [the longest x2 4.19 us: conv_taps(): window = padded[tap_row:tap_row + out_rows, tap_col:tap_col + out_cols, :]]
    ppermute x4 -> x0, waiting for transfers between devices: 4.79 us -> none  [shifted(): return lax.ppermute(block, axis, route)]
    reshape x5 -> x0, local copies, waits for them, and re-layouts: 4.07 us -> none  [the longest x1 3.75 us: per_device(): doubled = doubled.reshape(2 * tall_rows, 2 * columns, channels)]
  transfers between devices with their start and end apart: 4 -> 0, of which waited for: 2 -> 0; matrix products, arithmetic and copies ran while one was open for 2% -> 0% of each run, Pallas kernels for 0% -> 0%
where the time goes in v1:
time: 29 us; the launch traced here: 28.8 us
  Pallas kernels  25.7 us (89%)
  local copies, waits for them, and re-layouts  3.1 us (11%)
    pallas_call x1, Pallas kernels, per_device(): pl.pallas_call(functools.partial(kernel, n_view, rows, cols, chans), out_...  25.7 us
    unnamed x1, local copies, waits for them, and re-layouts  3.1 us

profile of v1, /device:TPU:0, one launch (start us, length us, event | category | flops | bytes accessed | tf_op | source)
XLA Modules:
  0.0 28.8 jit_solution(17400769464971270888)
XLA Ops:
  0.0 25.7 %shard_map.73 = bf16[8,2,128,512]{3,2,1,0:T(8,128)(2,1)} custom-call(bf16[8,64,512]{2,1,0:T(8,128)(2,1)} %lat_hbm.1, f32[1,512]{1,0:T(1,128)} %bitcast.14, f32[1,512]{1,0:T(1,128)} %bitcast.15, bf16[9,512,512]{2,1,0:T(8,128)(2,1)} %bitcast.12, f32[1,512]{1,0:T(1,128)} %bitcast.16, bf16[9,512,512]{2,1,0:T(8,128)(2,1)} %bitcast.13, f32[1,512]{1,0:T(1,128)} %bitcast.17), custom_call_target="tpu_custom_call" | custom-call | tf_op jit(solution)/shard_map/pallas_call | solution.py:266
  25.7 3.1 %copy.9 = bf16[16,128,512]{2,1,0:T(8,128)(2,1)} copy(bf16[16,128,512]{2,1,0:T(8,128)(2,1)} %bitcast.11) | data formatting | bytes 4194304

commit v2 on v1

--- a/solution.py
+++ b/solution.py
@@ -31,7 +31,6 @@
     views = n_view // slabs
     slab = me // views
     own = rows * cols
-    ext = (rows + 2) * cols
     has_up = slab > 0
     has_down = slab < slabs - 1
 
@@ -44,10 +43,10 @@
         pl.semaphore_signal(barrier, inc=1, device_id={"view": lax.rem(me + k, n_view)})
         return carry
 
-    lax.fori_loop(1, n_view, greet, 0)
+    lax.fori_loop(1, n_view, greet, 0, unroll=n_view <= 16)
 
     def w1_copy(t):
-        return pltpu.make_async_copy(w1_hbm.at[t], w1.at[t], w1_sem.at[t])
+        return pltpu.make_async_copy(w1_hbm.at[t], w1.at[:, pl.ds(t * chans, chans)], w1_sem.at[t])
 
     def w2_copy(t):
         return pltpu.make_async_copy(w2_hbm.at[t], w2.at[t], w2_sem.at[t])
@@ -94,7 +93,7 @@
         stat_copy(k).start()
         return carry
 
-    lax.fori_loop(1, n_view, send_stat, 0)
+    lax.fori_loop(1, n_view, send_stat, 0, unroll=n_view <= 16)
 
     up_copy = pltpu.make_async_remote_copy(
         src_ref=lat_hbm.at[pl.ds(0, 2)], dst_ref=lat.at[pl.ds(rows + 2, 2)],
@@ -114,72 +113,6 @@
     @pl.when(has_down)
     def _():
         down_copy.start()
-
-    pltpu.make_async_copy(stat_in, stat_in, stat_recv).wait()
-
-    total = stat[...]
-    total = total + jnp.sum(stat_in[...], axis=0)
-    entries = float(own * (chans // GROUPS) * n_view)
-    mean = total[:blocks] / entries
-    var = total[blocks:] / entries - mean * mean
-    inv = lax.rsqrt(var + EPSILON)
-
-    def one_row(v):
-        return jnp.concatenate([v[k : k + 1] for k in range(blocks)], axis=1)
-
-    scale = one_row(inv) * gain_ref[...]
-    offset = shift_ref[...] - one_row(mean) * scale
-
-    @pl.when(has_up)
-    def _():
-        down_copy.wait_recv()
-
-    @pl.when(has_down)
-    def _():
-        up_copy.wait_recv()
-
-    col = lax.broadcasted_iota(jnp.int32, (cols, chans), 0)
-
-    def left_of(x):
-        return jnp.where(col == 0, 0.0, pltpu.roll(x, 1, 0))
-
-    def right_of(x):
-        return jnp.where(col == cols - 1, 0.0, pltpu.roll(x, cols - 1, 0))
-
-    half_scale = scale * 0.5
-    half_offset = offset * 0.5
-
-    def activate(i, carry):
-        h = lat[i].astype(F32) * half_scale + half_offset
-        a = h + h * jnp.tanh(h)
-        place = slab * rows + i - 2
-        a = jnp.where(jnp.logical_and(place >= 0, place < H_LAT), a, 0.0)
-        at = pl.ds(pl.multiple_of(i * cols, cols), cols)
-        act[0, at] = left_of(a).astype(BF16)
-        act[1, at] = a.astype(BF16)
-        act[2, at] = right_of(a).astype(BF16)
-        return carry
-
-    lax.fori_loop(0, rows + 4, activate, 0)
-
-    def tap(t, carry):
-        w1_copy(t).wait()
-        r = t // 3
-        s = t - 3 * r
-        x = act[s, pl.ds(pl.multiple_of(r * cols, cols), ext)]
-        term = dot_nt(x, w1[t])
-
-        @pl.when(t == 0)
-        def _():
-            acc[...] = term
-
-        @pl.when(t > 0)
-        def _():
-            acc[...] += term
-
-        return carry
-
-    lax.fori_loop(0, 9, tap, 0)
 
     for t in range(9):
         w2_copy(t).wait()
@@ -198,6 +131,79 @@
 
     lax.fori_loop(0, chans // piece, fold_piece, 0)
 
+    pltpu.make_async_copy(stat_in, stat_in, stat_recv).wait()
+
+    total = stat[...]
+    total = total + jnp.sum(stat_in[...], axis=0)
+    entries = float(own * (chans // GROUPS) * n_view)
+    mean = total[:blocks] / entries
+    var = total[blocks:] / entries - mean * mean
+    inv = lax.rsqrt(var + EPSILON)
+
+    def one_row(v):
+        return jnp.concatenate([v[k : k + 1] for k in range(blocks)], axis=1)
+
+    scale = one_row(inv) * gain_ref[...]
+    offset = shift_ref[...] - one_row(mean) * scale
+
+    col = lax.broadcasted_iota(jnp.int32, (cols, chans), 0)
+
+    def left_of(x):
+        return jnp.where(col == 0, 0.0, pltpu.roll(x, 1, 0))
+
+    def right_of(x):
+        return jnp.where(col == cols - 1, 0.0, pltpu.roll(x, cols - 1, 0))
+
+    half_scale = scale * 0.5
+    half_offset = offset * 0.5
+
+    def activate(i, carry):
+        h = lat[i].astype(F32) * half_scale + half_offset
+        a = h + h * jnp.tanh(h)
+        place = slab * rows + i - 2
+        a = jnp.where(jnp.logical_and(place >= 0, place < H_LAT), a, 0.0)
+        at = pl.ds(pl.multiple_of(i * cols, cols), cols)
+        act[at, pl.ds(0, chans)] = left_of(a).astype(BF16)
+        act[at, pl.ds(chans, chans)] = a.astype(BF16)
+        act[at, pl.ds(2 * chans, chans)] = right_of(a).astype(BF16)
+        return carry
+
+    lax.fori_loop(2, rows + 2, activate, 0)
+    for t in range(9):
+        w1_copy(t).wait()
+    deep = 3 * chans
+    half = 256
+
+    def taps(windows, n):
+        lanes = pl.ds(n * half, half)
+        terms = [
+            dot_nt(
+                jnp.concatenate([act[pl.ds(first + r * cols, size)] for first, size in windows], axis=0),
+                w1[lanes, pl.ds(r * deep, deep)],
+            )
+            for r in range(3)
+        ]
+        return terms[0] + terms[1] + terms[2]
+
+    for n in range(chans // half):
+        acc[pl.ds(2 * cols, own - 2 * cols), pl.ds(n * half, half)] = taps([(2 * cols, own - 2 * cols)], n)
+
+    @pl.when(has_up)
+    def _():
+        down_copy.wait_recv()
+
+    @pl.when(has_down)
+    def _():
+        up_copy.wait_recv()
+
+    lax.fori_loop(0, 2, activate, 0)
+    lax.fori_loop(rows + 2, rows + 4, activate, 0)
+    ends = [(0, 2 * cols), (own, 2 * cols)]
+    for n in range(chans // half):
+        term = taps(ends, n)
+        for k, (first, size) in enumerate(ends):
+            acc[pl.ds(first, size), pl.ds(n * half, half)] = term[k * size : (k + 1) * size]
+
     bias1 = b1_ref[...]
 
     def mixed_row(i):
@@ -221,8 +227,8 @@
 
     width = 256
 
-    def out_tile(n, carry):
-        lanes = pl.ds(pl.multiple_of(n * width, width), width)
+    for n in range(chans // width):
+        lanes = pl.ds(n * width, width)
         head = pl.ds(0, own)
         base = dot_nt(lhs_m[0, head], fold[0, lanes]) + b2_ref[:, lanes]
         part[0] = base + dot_nt(lhs_m[1, head], fold[1, lanes])
@@ -235,15 +241,9 @@
                 value = part[q] + term if p else part[q] - term
                 for g in range(width // LANES):
                     wide[g, pl.ds(p * own * 2 + q, own, 2), :] = value[:, g * LANES : (g + 1) * LANES]
-        for p in range(2):
             for g in range(width // LANES):
                 tile = wide[g, pl.ds(p * own * 2, own * 2), :].astype(BF16)
-                out_ref[:, p, :, pl.ds(pl.multiple_of(n * width + g * LANES, LANES), LANES)] = tile.reshape(
-                    rows, 2 * cols, LANES
-                )
-        return carry
-
-    lax.fori_loop(0, chans // width, out_tile, 0)
+                out_ref[:, p, :, pl.ds(n * width + g * LANES, LANES)] = tile.reshape(rows, 2 * cols, LANES)
 
     pltpu.make_async_copy(stat_in, stat_in, stat_send).wait()
 
@@ -265,15 +265,15 @@
     hbm = pl.BlockSpec(memory_space=pl.ANY)
     out = pl.pallas_call(
         functools.partial(kernel, n_view, rows, cols, chans),
-        out_shape=jax.ShapeDtypeStruct((rows, 2, 2 * cols, chans), BF16),
+        out_shape=pltpu.VMEM((rows, 2, 2 * cols, chans), BF16),
         in_specs=[hbm, vmem, vmem, hbm, vmem, hbm, vmem],
         out_specs=vmem,
         scratch_shapes=[
             pltpu.VMEM((rows + 4, cols, chans), BF16),
-            pltpu.VMEM((9, chans, chans), BF16),
+            pltpu.VMEM((chans, 9 * chans), BF16),
             pltpu.VMEM((9, chans, chans), BF16),
             pltpu.VMEM((5, chans, chans), BF16),
-            pltpu.VMEM((3, (rows + 4) * cols, chans), BF16),
+            pltpu.VMEM(((rows + 4) * cols, 3 * chans), BF16),
             pltpu.VMEM(((rows + 2) * cols, chans), F32),
             pltpu.VMEM((3, own + cols, chans), BF16),
             pltpu.VMEM((3, own + cols, chans), BF16),

time: 29 us -> 19.9 us (0.69)
  Pallas kernels: 25.7 us -> 18.4 us
  local copies, waits for them, and re-layouts: 3.1 us -> 1.32 us
    pallas_call x1, Pallas kernels: 25.7 us -> 18.4 us  [per_device(): pl.pallas_call(functools.partial(kernel, n_view, rows, cols, chans), out_...]
    unnamed x1, local copies, waits for them, and re-layouts: 3.1 us -> 1.32 us
where the time goes in v2:
time: 19.9 us; the launch traced here: 19.7 us
  Pallas kernels  18.4 us (92%)
  local copies, waits for them, and re-layouts  1.32 us (7%)
    pallas_call x1, Pallas kernels, per_device(): pl.pallas_call(functools.partial(kernel, n_view, rows, cols, chans), out_...  18.4 us
    unnamed x1, local copies, waits for them, and re-layouts  1.32 us

profile of v2, /device:TPU:0, one launch (start us, length us, event | category | flops | bytes accessed | tf_op | source)
XLA Modules:
  0.0 19.7 jit_solution(5809296929743224100)
XLA Ops:
  0.0 18.4 %shard_map.73 = bf16[8,2,128,512]{3,2,1,0:T(8,128)(2,1)S(1)} custom-call(bf16[8,64,512]{2,1,0:T(8,128)(2,1)} %lat_hbm.1, f32[1,512]{1,0:T(1,128)} %bitcast.14, f32[1,512]{1,0:T(1,128)} %bitcast.15, bf16[9,512,512]{2,1,0:T(8,128)(2,1)} %bitcast.12, f32[1,512]{1,0:T(1,128)} %bitcast.16, bf16[9,512,512]{2,1,0:T(8,128)(2,1)} %bitcast.13, f32[1,512]{1,0:T(1,128)} %bitcast.17), custom_call_target="tpu_custom_call" | custom-call | tf_op jit(solution)/shard_map/pallas_call | solution.py:266
  18.4 1.3 %copy.9 = bf16[16,128,512]{2,1,0:T(8,128)(2,1)} copy(bf16[16,128,512]{2,1,0:T(8,128)(2,1)S(1)} %bitcast.11) | data formatting | bytes 4194304

commit v3 on v2

--- a/solution.py
+++ b/solution.py
@@ -96,12 +96,12 @@
     lax.fori_loop(1, n_view, send_stat, 0, unroll=n_view <= 16)
 
     up_copy = pltpu.make_async_remote_copy(
-        src_ref=lat_hbm.at[pl.ds(0, 2)], dst_ref=lat.at[pl.ds(rows + 2, 2)],
+        src_ref=lat.at[pl.ds(2, 2)], dst_ref=lat.at[pl.ds(rows + 2, 2)],
         send_sem=halo_send.at[0], recv_sem=halo_recv.at[0],
         device_id={"view": jnp.maximum(me - views, 0)},
     )
     down_copy = pltpu.make_async_remote_copy(
-        src_ref=lat_hbm.at[pl.ds(rows - 2, 2)], dst_ref=lat.at[pl.ds(0, 2)],
+        src_ref=lat.at[pl.ds(rows, 2)], dst_ref=lat.at[pl.ds(0, 2)],
         send_sem=halo_send.at[1], recv_sem=halo_recv.at[1],
         device_id={"view": jnp.minimum(me + views, n_view - 1)},
     )

time: 19.9 us -> 19.9 us (level)
  no operation moved by 1% of the time
where the time goes in v3:
time: 19.9 us; the launch traced here: 19.7 us
  Pallas kernels  18.4 us (92%)
  local copies, waits for them, and re-layouts  1.32 us (7%)
    pallas_call x1, Pallas kernels, per_device(): pl.pallas_call(functools.partial(kernel, n_view, rows, cols, chans), out_...  18.4 us
    unnamed x1, local copies, waits for them, and re-layouts  1.32 us

profile of v3, /device:TPU:0, one launch (start us, length us, event | category | flops | bytes accessed | tf_op | source)
XLA Modules:
  0.0 19.7 jit_solution(18445106245575641089)
XLA Ops:
  0.0 18.4 %shard_map.73 = bf16[8,2,128,512]{3,2,1,0:T(8,128)(2,1)S(1)} custom-call(bf16[8,64,512]{2,1,0:T(8,128)(2,1)} %lat_hbm.1, f32[1,512]{1,0:T(1,128)} %bitcast.14, f32[1,512]{1,0:T(1,128)} %bitcast.15, bf16[9,512,512]{2,1,0:T(8,128)(2,1)} %bitcast.12, f32[1,512]{1,0:T(1,128)} %bitcast.16, bf16[9,512,512]{2,1,0:T(8,128)(2,1)} %bitcast.13, f32[1,512]{1,0:T(1,128)} %bitcast.17), custom_call_target="tpu_custom_call" | custom-call | tf_op jit(solution)/shard_map/pallas_call | solution.py:266
  18.4 1.3 %copy.9 = bf16[16,128,512]{2,1,0:T(8,128)(2,1)} copy(bf16[16,128,512]{2,1,0:T(8,128)(2,1)S(1)} %bitcast.11) | data formatting | bytes 4194304
